TPU v7x, 32 devices: a 4x4x1 block of a 4x4x8 slice. The times are simulated.
32 devices in a mesh: batch: 1 (over z), head: 4 (over y), seq: 8 (over x, core).
Axes of the slice: x: 4, y: 4, z: 1, core: 2. Of those that a mesh axis runs over, the one named last changes fastest.
The devices are a block of a 4x4x8 slice.
Arguments:
- x_embed: bfloat16 [2048, 4096], P(('batch', 'seq'))
- positions: int32 [2048], P(('batch', 'seq'))
- w_q: bfloat16 [3, 4096, 32, 128], P(None, None, 'head')
- w_k: bfloat16 [3, 4096, 8, 128], P(None, None, 'head')
- w_v: bfloat16 [3, 4096, 8, 128], P(None, None, 'head')
- w_o: bfloat16 [3, 32, 128, 4096], P(None, 'head')
- w_gate: bfloat16 [3, 4096, 14336], P(None, None, 'head')
- w_up: bfloat16 [3, 4096, 14336], P(None, None, 'head')
- w_down: bfloat16 [3, 14336, 4096], P(None, 'head')
- norm_gain: bfloat16 [3, 4096], replicated
Outputs:
- output 1: bfloat16 [2048, 4096], P(('batch', 'seq'))
- output 2: bfloat16 [3, 2048, 8, 128], P(None, ('batch', 'seq'), 'head')
- output 3: bfloat16 [3, 2048, 8, 128], P(None, ('batch', 'seq'), 'head')
All inputs are finite; a program needn't handle non-finite values.
Results may differ from a plain program's by a relative error of at most 0.02.
Values are sent between devices in bfloat16 or wider.
A program may use at most 768 MiB of HBM per device.

v0:
```python
import math
import jax
import jax.numpy as jnp
from jax import lax
from jax.sharding import PartitionSpec as P

ROPE_BASE = 500000.0
EPS = 1e-5


def rms_norm(x_in, gain_row):
    x_f32 = x_in.astype(jnp.float32)
    inv_rms = lax.rsqrt(jnp.mean(x_f32 * x_f32, axis=-1, keepdims=True) + EPS)
    return (x_f32 * inv_rms * gain_row.astype(jnp.float32)).astype(jnp.bfloat16)


def rope_tables(positions, head_dim):
    half_dim = head_dim // 2
    inv_freq = ROPE_BASE ** (-(jnp.arange(half_dim, dtype=jnp.float32) * 2.0 / head_dim))
    angles = positions.astype(jnp.float32)[..., None] * inv_freq
    return jnp.cos(angles), jnp.sin(angles)


def apply_rope(heads_in, cos_t, sin_t):
    half_dim = heads_in.shape[-1] // 2
    heads_f32 = heads_in.astype(jnp.float32)
    first_half = heads_f32[..., :half_dim]
    second_half = heads_f32[..., half_dim:]
    cos_b = cos_t[..., None, :]
    sin_b = sin_t[..., None, :]
    rotated = jnp.concatenate([first_half * cos_b - second_half * sin_b, second_half * cos_b + first_half * sin_b], axis=-1)
    return rotated.astype(jnp.bfloat16)


def block_update(soft_state, q_rot, k_blk, v_blk, row_index, col_index, logit_scale):
    row_max, row_sum, accum_out = soft_state
    logits = jnp.einsum('qkgd,skd->qkgs', q_rot, k_blk, preferred_element_type=jnp.float32) * logit_scale
    allowed = (row_index[:, None] >= col_index[None, :])[:, None, None, :]
    logits = jnp.where(allowed, logits, -jnp.inf)
    new_max = jnp.maximum(row_max, jnp.max(logits, axis=-1))
    prob_f32 = jnp.exp(logits - new_max[..., None])
    rescale = jnp.exp(row_max - new_max)
    row_sum = row_sum * rescale + jnp.sum(prob_f32, axis=-1)
    pv_part = jnp.einsum('qkgs,skd->qkgd', prob_f32.astype(jnp.bfloat16), v_blk, preferred_element_type=jnp.float32)
    accum_out = accum_out * rescale[..., None] + pv_part
    return new_max, row_sum, accum_out


def passed_attention(q_rot, k_rot, v_heads, seq_count):
    tok_count, kv_local, group_size, head_dim = q_rot.shape
    my_index = lax.axis_index('seq')
    logit_scale = 1.0 / math.sqrt(head_dim)
    local_index = jnp.arange(tok_count)
    row_index = my_index * tok_count + local_index
    shift_pairs = [(sender, (sender + 1) % seq_count) for sender in range(seq_count)]
    stat_shape = (tok_count, kv_local, group_size)
    init_state = (jnp.full(stat_shape, -jnp.inf, jnp.float32), jnp.zeros(stat_shape, jnp.float32), jnp.zeros(stat_shape + (head_dim,), jnp.float32))
    first_state = block_update(init_state, q_rot, k_rot, v_heads, row_index, row_index, logit_scale)

    def pass_step(step_num, loop_carry):
        k_blk, v_blk, state_in = loop_carry
        k_blk = lax.ppermute(k_blk, 'seq', shift_pairs)
        v_blk = lax.ppermute(v_blk, 'seq', shift_pairs)
        src_index = (my_index - step_num) % seq_count
        col_index = src_index * tok_count + local_index
        return k_blk, v_blk, block_update(state_in, q_rot, k_blk, v_blk, row_index, col_index, logit_scale)

    final_carry = lax.fori_loop(1, seq_count, pass_step, (k_rot, v_heads, first_state))
    row_max, row_sum, accum_out = final_carry[2]
    attn_heads = (accum_out / row_sum[..., None]).astype(jnp.bfloat16)
    return attn_heads.reshape(tok_count, kv_local * group_size * head_dim)


def solution(mesh):
    seq_count = mesh.shape['seq']
    row_spec = P(('batch', 'seq'), None)
    pos_spec = P(('batch', 'seq'))
    head_spec = P(None, None, 'head', None)
    out_proj_spec = P(None, 'head', None, None)
    col_spec = P(None, None, 'head')
    down_spec = P(None, 'head', None)
    cache_spec = P(None, ('batch', 'seq'), 'head', None)

    def local_forward(x_loc, pos_loc, w_q, w_k, w_v, w_o, w_gate, w_up, w_down, norm_gain):
        tok_count, d_model = x_loc.shape
        layer_count = w_q.shape[0]
        q_local = w_q.shape[2]
        head_dim = w_q.shape[3]
        kv_local = w_k.shape[2]
        group_size = q_local // kv_local
        cos_t, sin_t = rope_tables(pos_loc, head_dim)
        x_cur = x_loc
        k_list = []
        v_list = []
        for layer in range(layer_count):
            normed = rms_norm(x_cur, norm_gain[layer])
            q_proj = jnp.dot(normed, w_q[layer].reshape(d_model, q_local * head_dim), preferred_element_type=jnp.float32).astype(jnp.bfloat16)
            k_proj = jnp.dot(normed, w_k[layer].reshape(d_model, kv_local * head_dim), preferred_element_type=jnp.float32).astype(jnp.bfloat16)
            v_proj = jnp.dot(normed, w_v[layer].reshape(d_model, kv_local * head_dim), preferred_element_type=jnp.float32).astype(jnp.bfloat16)
            q_rot = apply_rope(q_proj.reshape(tok_count, q_local, head_dim), cos_t, sin_t).reshape(tok_count, kv_local, group_size, head_dim)
            k_rot = apply_rope(k_proj.reshape(tok_count, kv_local, head_dim), cos_t, sin_t)
            v_heads = v_proj.reshape(tok_count, kv_local, head_dim)
            attn_heads = passed_attention(q_rot, k_rot, v_heads, seq_count)
            part_sum = jnp.dot(attn_heads, w_o[layer].reshape(q_local * head_dim, d_model), preferred_element_type=jnp.float32)
            gate_f32 = jnp.dot(normed, w_gate[layer], preferred_element_type=jnp.float32)
            up_f32 = jnp.dot(normed, w_up[layer], preferred_element_type=jnp.float32)
            hidden = (jax.nn.silu(gate_f32) * up_f32).astype(jnp.bfloat16)
            part_sum = part_sum + jnp.dot(hidden, w_down[layer], preferred_element_type=jnp.float32)
            update = lax.psum(part_sum, 'head').astype(jnp.bfloat16)
            x_cur = (x_cur.astype(jnp.float32) + update.astype(jnp.float32)).astype(jnp.bfloat16)
            k_list.append(k_rot)
            v_list.append(v_heads)
        return x_cur, jnp.stack(k_list), jnp.stack(v_list)

    return jax.shard_map(local_forward, mesh=mesh, in_specs=(row_spec, pos_spec, head_spec, head_spec, head_spec, out_proj_spec, col_spec, col_spec, down_spec, P(None, None)), out_specs=(row_spec, cache_spec, cache_spec), check_vma=False)
```

profile of v0, /device:TPU:103, one launch (start us, length us, event | category | flops | bytes accessed | tf_op | source)
XLA Modules:
  0.0 659.2 jit_solution(10652039128343109535)
XLA Ops:
  4.3 7.6 %fusion.230 = (bf16[1,4096,2,128]{3,2,1,0:T(2,128)(2,1)}, bf16[1,4096,2,128]{3,2,1,0:T(2,128)(2,1)S(1)}, bf16[1,4096,2,128]{3,2,1,0:T(2,128)(2,1)}) fusion(bf16[3,4096,2,128]{3,2,1,0:T(2,128)(2,1)} %param.19), kind=kLoop, calls=%fused_computation.223 | loop fusion | bytes 12582912 | tf_op jit(solution)/shard_map/slice | solution.py:98
  14.2 14.4 %fusion.228 = (bf16[1,4096,8,128]{3,2,1,0:T(8,128)(2,1)}, bf16[1,4096,8,128]{3,2,1,0:T(8,128)(2,1)S(1)}, bf16[1,4096,8,128]{3,2,1,0:T(8,128)(2,1)}) fusion(bf16[3,4096,8,128]{3,2,1,0:T(8,128)(2,1)} %param.18), kind=kLoop, calls=%fused_computation.221 | loop fusion | bytes 50331648 | tf_op jit(solution)/shard_map/slice | solution.py:97
  33.7 7.5 %fusion.229 = (bf16[1,4096,2,128]{3,2,1,0:T(2,128)(2,1)}, bf16[1,4096,2,128]{3,2,1,0:T(2,128)(2,1)S(1)}, bf16[1,4096,2,128]{3,2,1,0:T(2,128)(2,1)}) fusion(bf16[3,4096,2,128]{3,2,1,0:T(2,128)(2,1)} %param.20), kind=kLoop, calls=%fused_computation.222 | loop fusion | bytes 12582912 | tf_op jit(solution)/shard_map/slice | solution.py:99
  43.4 53.5 %while.72 = (s32[]{:T(128)}, bf16[256,2,128]{2,0,1:T(8,128)(2,1)S(1)}, bf16[256,2,128]{2,0,1:T(8,128)(2,1)S(1)}, f32[256,2,4]{0,2,1:T(4,128)S(1)}, f32[256,2,4]{...) while((s32[]{:T(128)}, ...), condition=%wide.region_6.7_spmd.clone, body=%wide.region_3.6_spmd.clone.sunk | while | flops 272699904 | bytes 11014498 | solution.py:68
  97.3 14.0 %fusion.227 = (bf16[1,8,128,4096]{3,2,1,0:T(8,128)(2,1)}, bf16[1,8,128,4096]{3,2,1,0:T(8,128)(2,1)S(1)}, bf16[1,8,128,4096]{3,2,1,0:T(8,128)(2,1)}) fusion(bf16[3,8,128,4096]{3,2,1,0:T(8,128)(2,1)} %param.21), kind=kLoop, calls=%fused_computation.220 | loop fusion | bytes 50331648 | tf_op jit(solution)/shard_map/slice | solution.py:104
  111.3 4.5 fusion.237
  115.8 14.6 %fusion.49 = f32[256,3584]{1,0:T(8,128)} fusion(bf16[3,4096,3584]{2,1,0:T(8,128)(2,1)} %param.22, bf16[256,4096]{1,0:T(8,128)(2,1)S(1)} %copy-done.2, f32[4096]{0:T(1024)S(1)} %bitcast.463, f32[256]{0:T(256)S(1)} %add_rsqrt_fusion.2), kind=kOutput, calls=%fused_computation.64 | convolution fusion | flops 7520387072 | bytes 35144704 | tf_op jit(solution)/shard_map/dot_general | solution.py:105
  130.4 15.4 %fusion.93.clone.5 = bf16[256,3584]{1,0:T(8,128)(2,1)} fusion(bf16[3,4096,3584]{2,1,0:T(8,128)(2,1)} %param.23, f32[256,3584]{1,0:T(8,128)} %fusion.49, bf16[256,4096]{1,0:T(8,128)(2,1)S(1)} %copy-done.2, f32[4096]{0:T(1024)S(1)} %bitcast.464, f32[256]{0:T(256)S(1)} %add_rsqrt_fusion.2), kind=kOutput, calls=%fused_computation.101.clone.clone.clone.2 | convolution fusion | flops 7525892096 | bytes 36979712 | tf_op jit(solution)/shard_map/dot_general | solution.py:106
  145.8 16.5 %fusion.78 = f32[256,4096]{1,0:T(8,128)} fusion(f32[256,4096]{1,0:T(8,128)} %fusion.237, bf16[3,3584,4096]{2,1,0:T(8,128)(2,1)} %param.24, bf16[256,3584]{1,0:T(8,128)(2,1)} %fusion.93.clone.5), kind=kOutput, calls=%fused_computation.96 | convolution fusion | flops 7517241344 | bytes 39583744 | tf_op jit(solution)/shard_map/dot_general | solution.py:108
  162.3 79.2 %all-reduce.3 = bf16[256,4096]{1,0:T(8,128)(2,1)S(1)} all-reduce(f32[256,4096]{1,0:T(8,128)} %fusion.78), channel_id=1, replica_groups=mesh['batch'=1,'head'=4,'seq'=8] {'head'}, use_global_device_ids=true, to_apply=%region_7.8 | all-reduce | flops 1048576 | bytes 6291456 | tf_op jit(solution)/shard_map/psum | solution.py:109
  245.4 15.4 %fusion.43 = f32[256,3584]{1,0:T(8,128)} fusion(bf16[3,4096,3584]{2,1,0:T(8,128)(2,1)} %param.22, bf16[256,4096]{1,0:T(8,128)(2,1)} %get-tuple-element.930, f32[4096]{0:T(1024)S(1)} %bitcast.455, f32[256]{0:T(256)S(1)} %add_rsqrt_fusion.1), kind=kOutput, calls=%fused_computation.58 | convolution fusion | flops 7520387072 | bytes 35144704 | tf_op jit(solution)/shard_map/dot_general | solution.py:105
  260.8 15.8 %fusion.90.clone.5 = bf16[256,3584]{1,0:T(8,128)(2,1)} fusion(bf16[3,4096,3584]{2,1,0:T(8,128)(2,1)} %param.23, f32[256,3584]{1,0:T(8,128)} %fusion.43, bf16[256,4096]{1,0:T(8,128)(2,1)S(1)} %copy-done.3, f32[4096]{0:T(1024)S(1)} %bitcast.456, f32[256]{0:T(256)S(1)} %add_rsqrt_fusion.1), kind=kOutput, calls=%fused_computation.100.clone.clone.clone.2 | convolution fusion | flops 7525892096 | bytes 36979712 | tf_op jit(solution)/shard_map/dot_general | solution.py:106
  276.6 5.8 fusion.159
  292.3 52.4 %while.73 = (s32[]{:T(128)}, bf16[256,2,128]{2,0,1:T(8,128)(2,1)S(1)}, bf16[256,2,128]{2,0,1:T(8,128)(2,1)S(1)}, f32[256,2,4]{0,2,1:T(4,128)S(1)}, f32[256,2,4]{...) while((s32[]{:T(128)}, ...), condition=%wide.region_14.15_spmd.clone, body=%wide.region_11.14_spmd.clone.sunk | while | flops 272699904 | bytes 11014498 | solution.py:68
  345.1 7.8 %fusion.238 = f32[256,4096]{1,0:T(8,128)} fusion(bf16[256,1024]{0,1:T(8,128)(2,1)S(1)} %bitcast.404, bf16[1024,4096]{1,0:T(8,128)(2,1)} %bitcast.391), kind=kOutput, calls=%fused_computation.231 | convolution fusion | flops 2147483648 | bytes 13107200 | tf_op jit(solution)/shard_map/dot_general | solution.py:104
  353.0 15.8 %fusion.81 = f32[256,4096]{1,0:T(8,128)} fusion(f32[256,4096]{1,0:T(8,128)} %fusion.238, bf16[3,3584,4096]{2,1,0:T(8,128)(2,1)} %param.24, bf16[256,3584]{1,0:T(8,128)(2,1)S(1)} %copy-done.26), kind=kOutput, calls=%fused_computation.97 | convolution fusion | flops 7517241344 | bytes 39583744 | tf_op jit(solution)/shard_map/dot_general | solution.py:108
  368.8 75.4 %all-reduce.4 = bf16[256,4096]{1,0:T(8,128)(2,1)} all-reduce(f32[256,4096]{1,0:T(8,128)} %fusion.81), channel_id=1, replica_groups=mesh['batch'=1,'head'=4,'seq'=8] {'head'}, use_global_device_ids=true, to_apply=%region_15.16 | all-reduce | flops 1048576 | bytes 6291456 | tf_op jit(solution)/shard_map/psum | solution.py:109
  457.4 18.5 %fusion.37 = f32[256,3584]{1,0:T(8,128)} fusion(bf16[3,4096,3584]{2,1,0:T(8,128)(2,1)} %param.22, bf16[256,4096]{1,0:T(8,128)(2,1)S(1)} %get-tuple-element.928, f32[4096]{0:T(1024)} %bitcast.450, f32[256]{0:T(256)S(1)} %add_rsqrt_fusion), kind=kOutput, calls=%fused_computation.52 | convolution fusion | flops 7520387072 | bytes 35144704 | tf_op jit(solution)/shard_map/dot_general | solution.py:105
  475.9 15.5 %fusion.87.clone.5 = bf16[256,3584]{1,0:T(8,128)(2,1)} fusion(bf16[3,4096,3584]{2,1,0:T(8,128)(2,1)} %param.23, f32[256,3584]{1,0:T(8,128)} %fusion.37, bf16[256,4096]{1,0:T(8,128)(2,1)S(1)} %get-tuple-element.928, f32[4096]{0:T(1024)S(1)} %bitcast.453, f32[256]{0:T(256)S(1)} %add_rsqrt_fusion), kind=kOutput, calls=%fused_computation.99.clone.clone.clone.2 | convolution fusion | flops 7525892096 | bytes 36979712 | tf_op jit(solution)/shard_map/dot_general | solution.py:106
  491.4 5.8 fusion.168
  500.3 52.6 %while.74 = (s32[]{:T(128)}, bf16[256,2,128]{2,0,1:T(8,128)(2,1)S(1)}, bf16[256,2,128]{2,0,1:T(8,128)(2,1)S(1)}, f32[256,2,4]{0,2,1:T(4,128)S(1)}, f32[256,2,4]{...) while((s32[]{:T(128)}, ...), condition=%wide.region_22.23_spmd.clone, body=%wide.region_19.22_spmd.clone.sunk | while | flops 272699904 | bytes 11014498 | solution.py:68
  553.4 7.9 %fusion.239 = f32[256,4096]{1,0:T(8,128)} fusion(bf16[256,1024]{0,1:T(8,128)(2,1)S(1)} %bitcast.403, bf16[1024,4096]{1,0:T(8,128)(2,1)} %bitcast.390), kind=kOutput, calls=%fused_computation.232 | convolution fusion | flops 2147483648 | bytes 13107200 | tf_op jit(solution)/shard_map/dot_general | solution.py:104
  561.2 15.8 %fusion.84 = f32[256,4096]{1,0:T(8,128)} fusion(f32[256,4096]{1,0:T(8,128)} %fusion.239, bf16[3,3584,4096]{2,1,0:T(8,128)(2,1)} %param.24, bf16[256,3584]{1,0:T(8,128)(2,1)S(1)} %copy-done.27), kind=kOutput, calls=%fused_computation.98 | convolution fusion | flops 7517241344 | bytes 39583744 | tf_op jit(solution)/shard_map/dot_general | solution.py:108
  577.1 78.0 %all-reduce.5 = bf16[256,4096]{1,0:T(8,128)(2,1)S(1)} all-reduce(f32[256,4096]{1,0:T(8,128)} %fusion.84), channel_id=1, replica_groups=mesh['batch'=1,'head'=4,'seq'=8] {'head'}, use_global_device_ids=true, to_apply=%region_23.24 | all-reduce | flops 1048576 | bytes 6291456 | tf_op jit(solution)/shard_map/psum | solution.py:109
  (451 shorter events, 204.5 us)
Async XLA Ops:
  44.3 3.3 collective-permute-start.1
  48.6 5.7 collective-permute-start
  52.3 3.3 collective-permute-start.1
  56.6 5.7 collective-permute-start
  60.4 3.3 collective-permute-start.1
  64.6 5.7 collective-permute-start
  72.7 5.7 collective-permute-start
  80.7 5.7 collective-permute-start
  84.4 3.3 collective-permute-start.1
  88.7 5.7 collective-permute-start
  92.4 3.3 collective-permute-start.1
  296.6 5.7 collective-permute-start.2
  300.4 3.3 collective-permute-start.3
  304.6 5.7 collective-permute-start.2
  312.6 5.7 collective-permute-start.2
  320.6 5.7 collective-permute-start.2
  328.7 5.7 collective-permute-start.2
  336.7 5.7 collective-permute-start.2
  504.8 5.7 collective-permute-start.4
  512.8 5.7 collective-permute-start.4
  520.8 5.7 collective-permute-start.4
  528.8 5.7 collective-permute-start.4
  536.9 5.7 collective-permute-start.4
  544.9 5.7 collective-permute-start.4
  (46 other events, 552.0 us)
where the time goes:
time: 669 us; the launch traced here: 659 us
  blocking collectives  233 us (35%)
  matrix products  219 us (33%)
  starting transfers between devices  70.2 us (10%)
  local copies, waits for them, and re-layouts  53.7 us (8%)
  waiting for transfers between devices  47.9 us (7%)
  other arithmetic  32.2 us (5%)
    psum x3, blocking collectives, local_forward(): update = lax.psum(part_sum, 'head').astype(jnp.bfloat16)  233 us
    ppermute x21, starting transfers between devices, pass_step(): k_blk = lax.ppermute(k_blk, 'seq', shift_pairs)  68.7 us
    dot_general x3, matrix products, local_forward(): jnp.dot(normed, w_gate[layer], preferred_element_type=jnp.float32)  48.5 us
    dot_general x3, matrix products, local_forward(): jnp.dot(hidden, w_down[layer], preferred_element_type=jnp.float32)  48.2 us
    dot_general x3, matrix products, local_forward(): up_f32 = jnp.dot(normed, w_up[layer], preferred_element_type=jnp.float32)  46.7 us
    ppermute x21, waiting for transfers between devices, pass_step(): k_blk = lax.ppermute(k_blk, 'seq', shift_pairs)  36.8 us
    dot_general x24, matrix products, block_update(): jnp.einsum('qkgs,skd->qkgd', prob_f32.astype(jnp.bfloat16), v_blk, prefer...  21.2 us
    dot_general x3, matrix products, local_forward(): jnp.dot(attn_heads, w_o[layer].reshape(q_local * head_dim, d_model), pref...  20.2 us
  transfers between devices with their start and end apart: 42, of which 42 were waited for; matrix products, arithmetic and copies ran while one was open for 3% of the time, Pallas kernels for 0%

commit v1 on v0

v1 whole, which is shorter than its diff:
```python
import functools
import math
import jax
import jax.numpy as jnp
from jax import lax
from jax.experimental import pallas as pl
from jax.experimental.pallas import tpu as pltpu
from jax.sharding import PartitionSpec as P

ROPE_BASE = 500000.0
EPS = 1e-5
F32 = jnp.float32
BF16 = jnp.bfloat16
MESH = pl.DeviceIdType.MESH

NSTREAM = 4
NGUBUF = 3
NWDBUF = 3


def rope_tables(positions, head_dim):
    half_dim = head_dim // 2
    inv_freq = ROPE_BASE ** (-(jnp.arange(half_dim, dtype=F32) * 2.0 / head_dim))
    angles = positions.astype(F32)[..., None] * inv_freq
    cos_t, sin_t = jnp.cos(angles), jnp.sin(angles)
    return jnp.stack([jnp.concatenate([cos_t, cos_t], -1), jnp.concatenate([-sin_t, sin_t], -1)])


def decoder_kernel(dims, x_h, cs_h, wqkv_h, wo_h, wg_h, wu_h, wd_h, gain_v, xout_h, kvout_h,
                   X, H, QKVS, Q, ATT, HID, G, PS, PAIR, RS, TAB, KV, GU, WD, WO, WQKV, MX, LS, ACC,
                   s_xin, s_xs, s_xr, s_tab, s_gu, s_wd, s_wo, s_wqkv, s_ps, s_pr, s_rss, s_rsr, s_ags, s_agr,
                   s_fws, s_fwr, s_kvs, s_kvr, s_cl, s_cs, s_cr, s_out):
    L, T, D, NY, NX, GH, HD, FF, FT, BW = (dims[k] for k in ('L', 'T', 'D', 'NY', 'NX', 'GH', 'HD', 'FF', 'FT', 'BW'))
    NB = 2 * NY
    NGU = FF // FT
    QW = GH * HD
    NQ = (QW + 2 * HD) // (2 * HD)
    NS = NSTREAM
    R = T // NS
    NE = (2 * NY - 1) * NS
    scale = 1.0 / math.sqrt(HD)

    y = lax.axis_index('head')
    s = lax.axis_index('seq')
    c = lax.rem(s, 2)
    xx = lax.div(s, 2)
    partner = {'seq': s + 1 - 2 * c}
    own0 = c * NY
    oth0 = (1 - c) * NY

    def rcopy(src, dst, ss, rs, dev):
        return pltpu.make_async_remote_copy(src_ref=src, dst_ref=dst, send_sem=ss, recv_sem=rs, device_id=dev, device_id_type=MESH)

    def lcopy(src, dst, sem):
        return pltpu.make_async_copy(src, dst, sem)

    def gu_copies(i):
        slot = lax.rem(i, NGUBUF)
        hs = lax.div(i, NGU)
        n = lax.rem(i, NGU)
        l = lax.div(hs, 2)
        cols = pl.ds(pl.multiple_of(c * FF + n * FT, FT), FT)
        return (lcopy(wg_h.at[l, :, cols], GU.at[slot, 0], s_gu.at[slot, 0]),
                lcopy(wu_h.at[l, :, cols], GU.at[slot, 1], s_gu.at[slot, 1]))

    def block_of(n):
        return jnp.where(n < NY, oth0 + n, own0 + lax.rem(y + 1 + n, NY))

    def wd_copy(i):
        slot = lax.rem(i, NWDBUF)
        hs = lax.div(i, NB)
        n = lax.rem(i, NB)
        l = lax.div(hs, 2)
        rows = pl.ds(pl.multiple_of(c * FF, FT), FF)
        cols = pl.ds(pl.multiple_of(block_of(n) * BW, BW), BW)
        return lcopy(wd_h.at[l, rows, cols], WD.at[slot], s_wd.at[slot])

    def wo_copy(l):
        return lcopy(wo_h.at[l, pl.ds(pl.multiple_of(c * QW, QW), QW), :], WO, s_wo.at[0])

    def wqkv_copy(l):
        return lcopy(wqkv_h.at[l], WQKV, s_wqkv.at[0])

    wqkv_copy(0).start()
    for i in range(NGUBUF):
        for cp in gu_copies(i):
            cp.start()
    for i in range(NWDBUF):
        wd_copy(i).start()
    wo_copy(0).start()

    barrier = pltpu.get_barrier_semaphore()
    peers = [partner, {'head': lax.rem(y + 1, NY)}, {'head': lax.rem(y + NY - 1, NY)}]
    peers += [{'seq': lax.rem(s + 2 * d, 2 * NX)} for d in range(1, NX)]
    for peer in peers:
        pl.semaphore_signal(barrier, inc=1, device_id=peer, device_id_type=MESH)
    pl.semaphore_wait(barrier, len(peers))

    def xin_local(b):
        return lcopy(x_h.at[:, pl.ds(b * BW, BW)], X.at[c, b], s_xin.at[b])

    def xin_remote(b):
        return rcopy(x_h.at[:, pl.ds(b * BW, BW)], X.at[c, b], s_xs.at[b], s_xr.at[b], partner)

    def tab_local():
        return lcopy(cs_h, TAB.at[c], s_tab.at[0])

    def tab_remote():
        return rcopy(cs_h, TAB.at[c], s_tab.at[1], s_tab.at[2], partner)

    for b in range(NB):
        xin_remote(b).start()
        xin_local(b).start()
    tab_remote().start()
    tab_local().start()
    for b in range(NB):
        xin_local(b).wait()
        xin_remote(b).wait()
    tab_local().wait()
    tab_remote().wait()

    def rows_of(st):
        return pl.ds(pl.multiple_of(st * R, R), R)

    def sign_of(st):
        return 1 - 2 * lax.rem(st, 2)

    def ring_dev(st):
        return {'head': lax.rem(y + sign_of(st) + NY, NY)}

    def blk_at(st, k):
        return lax.rem(y - sign_of(st) * k + 2 * NY, NY)

    def pair_copy(j, bb):
        return rcopy(PS.at[j, oth0 + bb], PAIR.at[j, bb], s_ps.at[j, bb], s_pr.at[j, bb], partner)

    def rs_copy(j, t, st):
        return rcopy(PS.at[j, own0 + blk_at(st, 1 + t), rows_of(st)], RS.at[j, t, rows_of(st)],
                     s_rss.at[j, t, st], s_rsr.at[j, t, st], ring_dev(st))

    def ag_copy(j, t, st):
        ref = X.at[j, own0 + blk_at(st, t), rows_of(st)]
        return rcopy(ref, ref, s_ags.at[j, t, st], s_agr.at[j, t, st], ring_dev(st))

    def fw_copy(j, t, st):
        ref = X.at[j, own0 + blk_at(st, t), rows_of(st)]
        return rcopy(ref, ref, s_fws.at[j, t, st], s_fwr.at[j, t, st], partner)

    def service(j, e):
        kind = lax.div(e, NS)
        st = lax.rem(e, NS)
        rows = rows_of(st)

        @pl.when(e == 0)
        def _():
            for bb in range(NY):
                pair_copy(j, bb).wait_recv()

        @pl.when(kind == 0)
        def _():
            bb = blk_at(st, 1)
            PS[j, own0 + bb, rows] += PAIR[j, bb, rows]
            rs_copy(j, 0, st).start()

        @pl.when((kind >= 1) & (kind < NY - 1))
        def _():
            t = kind - 1
            rs_copy(j, t, st).wait_recv()
            bb = blk_at(st, t + 2)
            PS[j, own0 + bb, rows] = PS[j, own0 + bb, rows] + PAIR[j, bb, rows] + RS[j, t, rows]
            rs_copy(j, t + 1, st).start()

        @pl.when(kind == NY - 1)
        def _():
            rs_copy(j, NY - 2, st).wait_recv()
            total = PS[j, own0 + y, rows] + PAIR[j, y, rows] + RS[j, NY - 2, rows]
            upd = total.astype(BF16).astype(F32)
            X[j, own0 + y, rows] = (X[j, own0 + y, rows].astype(F32) + upd).astype(BF16)
            ag_copy(j, 0, st).start()
            fw_copy(j, 0, st).start()

        @pl.when((kind >= NY) & (kind < 2 * NY - 1))
        def _():
            t = kind - NY
            ag_copy(j, t, st).wait_recv()

            @pl.when(t < NY - 2)
            def _():
                ag_copy(j, t + 1, st).start()
            fw_copy(j, t + 1, st).start()

    def drain(j, e0):
        def body(e, carry):
            service(j, e)
            return carry
        lax.fori_loop(e0, NE, body, 0)
        for bb in range(NY):
            pair_copy(j, bb).wait_send()

        def ends(st, carry):
            for t in range(NY):
                fw_copy(j, t, st).wait_recv()
            for t in range(NY - 1):
                rs_copy(j, t, st).wait_send()
                ag_copy(j, t, st).wait_send()
            for t in range(NY):
                fw_copy(j, t, st).wait_send()
            return carry
        lax.fori_loop(0, NS, ends, 0)

    def norm(j, l, slot):
        RG = T // 4

        def body(r, carry):
            rows = pl.ds(pl.multiple_of(r * RG, RG), RG)
            ssq = jnp.zeros((RG, BW), F32)
            for b in range(NB):
                xb = X[j, b, rows, :].astype(F32)
                ssq = ssq + xb * xb
            inv = lax.rsqrt(jnp.sum(ssq, axis=-1, keepdims=True) * (1.0 / D) + EPS)
            for b in range(NB):
                xb = X[j, b, rows, :].astype(F32)
                H[rows, b * BW:(b + 1) * BW] = (xb * inv * gain_v[l, :, b * BW:(b + 1) * BW]).astype(BF16)
            slot(r)
            return carry
        lax.fori_loop(0, 4, body, 0)

    def push_copy(j, l, d):
        g = 2 * xx + j
        return rcopy(KV.at[l, g], KV.at[l, g], s_kvs.at[j, d - 1], s_kvr.at[l * (2 * NX) + g], {'seq': lax.rem(s + 2 * d, 2 * NX)})

    def recv_wait(l, g):
        rcopy(KV.at[l, g], KV.at[l, g], s_kvs.at[0, 0], s_kvr.at[l * (2 * NX) + g], partner).wait_recv()

    def cache_local(l, j):
        return lcopy(KV.at[l, 2 * xx + j], kvout_h.at[l, c], s_cl.at[l])

    def cache_remote(l, j):
        return rcopy(KV.at[l, 2 * xx + j], kvout_h.at[l, c], s_cs.at[l], s_cr.at[l], partner)

    def qkv(j, l, slot):
        def body(n, carry):
            cols = pl.ds(pl.multiple_of(n * 2 * HD, 2 * HD), 2 * HD)
            QKVS[n] = jnp.dot(H[...], WQKV[:, cols], preferred_element_type=F32).astype(BF16)
            slot(n)
            return carry
        lax.fori_loop(0, NQ, body, 0)
        g = 2 * xx + j

        def rot(val):
            vf = val.astype(F32)
            return (vf * TAB[j, 0] + pltpu.roll(vf, HD // 2, 1) * TAB[j, 1]).astype(BF16)
        KV[l, g, 0] = rot(QKVS[NQ - 1, :, 0:HD])
        KV[l, g, 1] = QKVS[NQ - 1, :, HD:2 * HD]
        for d in range(1, NX):
            @pl.when(xx + d < NX)
            def _():
                push_copy(j, l, d).start()

        @pl.when(c == j)
        def _():
            cache_local(l, j).start()

        @pl.when(c != j)
        def _():
            cache_remote(l, j).start()
        for h in range(GH):
            Q[j, h] = rot(QKVS[h // 2, :, (h % 2) * HD:(h % 2 + 1) * HD])

    def push_done(j, l):
        for d in range(1, NX):
            @pl.when(xx + d < NX)
            def _():
                push_copy(j, l, d).wait_send()

    def attention(j, l, slot):
        g = 2 * xx + j
        nt = (((1,), (1,)), ((), ()))

        row_i = lax.broadcasted_iota(jnp.int32, (T, T), 0)
        col_i = lax.broadcasted_iota(jnp.int32, (T, T), 1)
        for h in range(GH):
            sc = lax.dot_general(Q[j, h], KV[l, g, 0], nt, preferred_element_type=F32) * scale
            sc = jnp.where(row_i >= col_i, sc, -jnp.inf)
            m = jnp.max(sc, axis=1, keepdims=True)
            p = jnp.exp(sc - m)
            MX[h] = jnp.broadcast_to(m, (T, HD))
            LS[h] = jnp.broadcast_to(jnp.sum(p, axis=1, keepdims=True), (T, HD))
            ACC[h] = jnp.dot(p.astype(BF16), KV[l, g, 1], preferred_element_type=F32)
        slot(0)

        def body(i, carry):
            if j == 0:
                gi = jnp.where(i < xx, 2 * i, 2 * (i - xx) + 1)
                recv_wait(l, gi)
            else:
                gi = i
            for h in range(GH):
                sc = lax.dot_general(Q[j, h], KV[l, gi, 0], nt, preferred_element_type=F32) * scale
                m_old = MX[h]
                m_new = jnp.maximum(m_old, jnp.max(sc, axis=1, keepdims=True))
                p = jnp.exp(sc - jnp.concatenate([m_new] * (T // HD), axis=1))
                alpha = jnp.exp(m_old - m_new)
                MX[h] = m_new
                LS[h] = LS[h] * alpha + jnp.sum(p, axis=1, keepdims=True)
                ACC[h] = ACC[h] * alpha + jnp.dot(p.astype(BF16), KV[l, gi, 1], preferred_element_type=F32)
            slot(i + 1)
            return carry
        lax.fori_loop(0, 2 * xx + j, body, 0)
        for h in range(GH):
            ATT[:, h * HD:(h + 1) * HD] = (ACC[h] / LS[h]).astype(BF16)

    def gate_up(j, l, slot):
        def body(n, carry):
            i = (2 * l + j) * NGU + n
            sl = lax.rem(i, NGUBUF)
            cg, cu = gu_copies(i)
            cg.wait()
            G[...] = jnp.dot(H[...], GU[sl, 0], preferred_element_type=F32)
            slot(2 * n)
            cu.wait()
            up = jnp.dot(H[...], GU[sl, 1], preferred_element_type=F32)
            gate = G[...]
            HID[:, pl.ds(pl.multiple_of(n * FT, FT), FT)] = (gate * jax.nn.sigmoid(gate) * up).astype(BF16)

            @pl.when(i + NGUBUF < 2 * L * NGU)
            def _():
                for cp in gu_copies(i + NGUBUF):
                    cp.start()
            slot(2 * n + 1)
            return carry
        lax.fori_loop(0, NGU, body, 0)

    def o_tile(blk):
        cols = pl.ds(pl.multiple_of(blk * BW, BW), BW)
        return jnp.dot(ATT[...], WO[:, cols], preferred_element_type=F32)

    def send_pair(j, n):
        @pl.when(n < NY)
        def _():
            pair_copy(j, n).start()

    def down(j, l, with_o, slot):
        def body(n, carry):
            i = (2 * l + j) * NB + n
            sl = lax.rem(i, NWDBUF)
            blk = block_of(n)
            wd_copy(i).wait()
            val = jnp.dot(HID[...], WD[sl], preferred_element_type=F32)
            if with_o:
                val = val + o_tile(blk)
            PS[j, blk] = val

            @pl.when(i + NWDBUF < 2 * L * NB)
            def _():
                wd_copy(i + NWDBUF).start()
            if with_o:
                send_pair(j, n)
            slot(n)
            return carry
        lax.fori_loop(0, NB, body, 0)

    def o_proj(j, l):
        def body(n, carry):
            blk = block_of(n)
            PS[j, blk] += o_tile(blk)
            send_pair(j, n)
            return carry
        lax.fori_loop(0, NB, body, 0)

    def layer(l, carry):
        def sv1(e):
            @pl.when((l > 0) & (e < NE))
            def _():
                service(1, e)

        def sv0(e):
            @pl.when(e < NE)
            def _():
                service(0, e)

        norm(0, l, lambda k: sv1(k))
        wqkv_copy(l).wait()
        qkv(0, l, lambda k: sv1(4 + k))
        e1 = 4 + NQ
        gate_up(0, l, lambda k: sv1(e1 + k))
        down(0, l, False, lambda k: sv1(e1 + 2 * NGU + k))

        @pl.when(l > 0)
        def _():
            drain(1, e1 + 2 * NGU + NB)

        norm(1, l, lambda k: None)
        qkv(1, l, lambda k: None)

        @pl.when(l + 1 < L)
        def _():
            wqkv_copy(l + 1).start()
        attention(0, l, lambda k: None)
        wo_copy(l).wait()
        o_proj(0, l)

        gate_up(1, l, lambda k: sv0(k))
        e0 = 2 * NGU
        attention(1, l, lambda k: sv0(e0 + k))
        e0 = e0 + 2 * xx + 2
        down(1, l, True, lambda k: sv0(e0 + k))

        @pl.when(l + 1 < L)
        def _():
            wo_copy(l + 1).start()
        drain(0, e0 + NB)
        push_done(0, l)
        push_done(1, l)
        return carry

    lax.fori_loop(0, L, layer, 0)
    drain(1, 0)

    for b in range(NB):
        lcopy(X.at[c, b], xout_h.at[:, pl.ds(b * BW, BW)], s_out.at[b]).start()
    for b in range(NB):
        lcopy(X.at[c, b], xout_h.at[:, pl.ds(b * BW, BW)], s_out.at[b]).wait()
    for l in range(L):
        cache_local(l, 0).wait()
        cache_remote(l, 0).wait()


def solution(mesh):
    NY = mesh.shape['head']
    NX = mesh.shape['seq'] // 2
    row_spec = P(('batch', 'seq'), None)
    pos_spec = P(('batch', 'seq'))
    head_spec = P(None, None, 'head', None)
    out_proj_spec = P(None, 'head', None, None)
    col_spec = P(None, None, 'head')
    down_spec = P(None, 'head', None)
    cache_spec = P(None, ('batch', 'seq'), 'head', None)

    def local_forward(x_loc, pos_loc, w_q, w_k, w_v, w_o, w_gate, w_up, w_down, norm_gain):
        T, D = x_loc.shape
        L, _, q_local, HD = w_q.shape
        GH = q_local // 2
        FF = w_gate.shape[2] // 2
        BW = D // (2 * NY)
        FT = 256 if FF % 256 == 0 else 128
        dims = dict(L=L, T=T, D=D, NY=NY, NX=NX, GH=GH, HD=HD, FF=FF, FT=FT, BW=BW)
        core = lax.rem(lax.axis_index('seq'), 2)
        wq_c = lax.dynamic_slice_in_dim(w_q, core * GH, GH, 2).reshape(L, D, GH * HD)
        wk_c = lax.dynamic_slice_in_dim(w_k, core, 1, 2).reshape(L, D, HD)
        wv_c = lax.dynamic_slice_in_dim(w_v, core, 1, 2).reshape(L, D, HD)
        wqkv = jnp.concatenate([wq_c, wk_c, wv_c], axis=2)
        wo = w_o.reshape(L, q_local * HD, D)
        gain = norm_gain.astype(F32).reshape(L, 1, D)
        tab = rope_tables(pos_loc, HD)
        QW = GH * HD
        NB = 2 * NY
        NQ = (QW + 2 * HD) // (2 * HD)
        any_spec = pl.BlockSpec(memory_space=pl.ANY)
        dma = pltpu.SemaphoreType.DMA
        V = pltpu.VMEM
        scratch = [
            V((2, NB, T, BW), BF16), V((T, D), BF16), V((NQ, T, 2 * HD), BF16), V((2, GH, T, HD), BF16), V((T, QW), BF16),
            V((T, FF), BF16), V((T, FT), F32), V((2, NB, T, BW), F32), V((2, NY, T, BW), F32), V((2, NY - 1, T, BW), F32),
            V((2, 2, T, HD), F32), V((L, 2 * NX, 2, T, HD), BF16), V((NGUBUF, 2, D, FT), BF16), V((NWDBUF, FF, BW), BF16),
            V((QW, D), BF16), V((D, QW + 2 * HD), BF16), V((GH, T, HD), F32), V((GH, T, HD), F32), V((GH, T, HD), F32),
            dma((NB,)), dma((NB,)), dma((NB,)), dma((3,)), dma((NGUBUF, 2)), dma((NWDBUF,)), dma((1,)), dma((1,)),
            dma((2, NY)), dma((2, NY)), dma((2, NY - 1, NSTREAM)), dma((2, NY - 1, NSTREAM)),
            dma((2, NY - 1, NSTREAM)), dma((2, NY - 1, NSTREAM)), dma((2, NY, NSTREAM)), dma((2, NY, NSTREAM)),
            dma((2, NX)), dma((L * 2 * NX,)), dma((L,)), dma((L,)), dma((L,)), dma((NB,)),
        ]
        x_out, kv = pl.pallas_call(
            functools.partial(decoder_kernel, dims),
            out_shape=(jax.ShapeDtypeStruct((T, D), BF16), jax.ShapeDtypeStruct((L, 2, 2, T, HD), BF16)),
            in_specs=[any_spec] * 7 + [pl.BlockSpec(memory_space=pltpu.VMEM)],
            out_specs=(any_spec, any_spec),
            scratch_shapes=scratch,
            compiler_params=pltpu.CompilerParams(collective_id=0, has_side_effects=True, vmem_limit_bytes=67043328),
            name='decoder',
        )(x_loc, tab, wqkv, wo, w_gate, w_up, w_down, gain)
        kv = jnp.transpose(kv, (2, 0, 3, 1, 4))
        return x_out, kv[0], kv[1]

    return jax.shard_map(local_forward, mesh=mesh, in_specs=(row_spec, pos_spec, head_spec, head_spec, head_spec, out_proj_spec, col_spec, col_spec, down_spec, P(None, None)), out_specs=(row_spec, cache_spec, cache_spec), check_vma=False)
```

time: 669 us -> 381 us (0.57); the launches traced: 659 us -> 380 us
  Pallas kernels: 0 us -> 295 us
  blocking collectives: 233 us -> 0 us
  matrix products: 219 us -> 0 us
  starting transfers between devices: 70.2 us -> 0 us
  waiting for transfers between devices: 47.9 us -> 0 us
  other arithmetic: 32.2 us -> 8.97 us
  local copies, waits for them, and re-layouts: 53.7 us -> 75 us
    pallas_call x0 -> x1, Pallas kernels: none -> 295 us  [local_forward(): pl.pallas_call(functools.partial(decoder_kernel, dims), out_shape=(jax.Sh...]
    psum x3 -> x0, blocking collectives: 233 us -> none  [local_forward(): update = lax.psum(part_sum, 'head').astype(jnp.bfloat16)]
    dot_general x69 -> x0, matrix products: 219 us -> none  [the longest x3 48.5 us: local_forward(): jnp.dot(normed, w_gate[layer], preferred_element_type=jnp.float32)]
    ppermute x42 -> x0, starting transfers between devices: 70.2 us -> none  [the longest x21 68.7 us: pass_step(): k_blk = lax.ppermute(k_blk, 'seq', shift_pairs)]
    ppermute x42 -> x0, waiting for transfers between devices: 47.9 us -> none  [the longest x21 36.8 us: pass_step(): k_blk = lax.ppermute(k_blk, 'seq', shift_pairs)]
    slice x7 -> x0, local copies, waits for them, and re-layouts: 43.5 us -> none  [the longest x1 14.4 us: local_forward(): w_q[layer].reshape(d_model, q_local * head_dim)]
    dynamic_slice x0 -> x2, local copies, waits for them, and re-layouts: none -> 29 us  [the longest x1 14.6 us: local_forward(): wv_c = lax.dynamic_slice_in_dim(w_v, core, 1, 2).reshape(L, D, HD)]
    unnamed x72 -> x16, local copies, waits for them, and re-layouts: 7.93 us -> 27.6 us
  transfers between devices with their start and end apart: 42 -> 0, of which waited for: 42 -> 0; matrix products, arithmetic and copies ran while one was open for 3% -> 0% of each run, Pallas kernels for 0% -> 0%
where the time goes in v1:
time: 381 us; the launch traced here: 380 us
  Pallas kernels  295 us (77%)
  local copies, waits for them, and re-layouts  75 us (20%)
  other arithmetic  8.97 us (2%)
    pallas_call x1, Pallas kernels, local_forward(): pl.pallas_call(functools.partial(decoder_kernel, dims), out_shape=(jax.Sh...  295 us
    unnamed x16, local copies, waits for them, and re-layouts  27.6 us
    reshape x1, local copies, waits for them, and re-layouts, local_forward(): lax.dynamic_slice_in_dim(w_q, core * GH, GH, 2).reshape(L, D, GH * HD)  16.6 us
    dynamic_slice x1, local copies, waits for them, and re-layouts, local_forward(): wv_c = lax.dynamic_slice_in_dim(w_v, core, 1, 2).reshape(L, D, HD)  14.6 us
    dynamic_slice x1, local copies, waits for them, and re-layouts, local_forward(): lax.dynamic_slice_in_dim(w_q, core * GH, GH, 2).reshape(L, D, GH * HD)  14.4 us

profile of v1, /device:TPU:103, one launch (start us, length us, event | category | flops | bytes accessed | tf_op | source)
XLA Modules:
  0.0 379.8 jit_solution(6990516586474442295)
XLA Ops:
  0.6 14.4 %constant_dynamic-slice_fusion.2 = bf16[3,4096,4,128]{3,2,1,0:T(4,128)(2,1)} fusion(bf16[3,4096,8,128]{3,2,1,0:T(8,128)(2,1)} %param.12, s32[]{:T(128)S(6)} %select_n.7), kind=kLoop, calls=%fused_computation.13 | loop fusion | bytes 25165828 | tf_op jit(solution)/shard_map/dynamic_slice | solution.py:449
  15.0 20.0 %copy.21 = bf16[3,4096,4,128]{1,3,2,0:T(8,128)(2,1)} copy(bf16[3,4096,4,128]{3,2,1,0:T(4,128)(2,1)} %constant_dynamic-slice_fusion.2) | data formatting | bytes 25165824
  35.0 16.6 %copy.18 = bf16[3,4096,512]{2,1,0:T(8,128)(2,1)} copy(bf16[3,4096,512]{1,2,0:T(8,128)(2,1)} %bitcast.17) | data formatting | bytes 25165824 | tf_op jit(solution)/shard_map/reshape | solution.py:449
  51.6 0.0 slice-start
  51.6 0.0 slice-start.1
  51.6 14.6 %constant_dynamic-slice_fusion = (bf16[3,4096,1,128]{3,2,1,0:T(2,128)(2,1)S(1)}, bf16[3,4096,1,128]{3,2,1,0:T(2,128)(2,1)S(1)}) fusion(bf16[3,4096,2,128]{3,2,1,0:T(2,128)(2,1)} %param.14, s32[]{:T(128)S(6)} %select_n.8, bf16[3,4096,2,128]{3,2,1,0:T(2,128)(2,1)} %param.13), kind=kLoop, calls=%fused_computation.11 | loop fusion | bytes 12582916 | tf_op jit(solution)/shard_map/dynamic_slice | solution.py:451
  66.2 0.0 slice-start.2
  66.2 0.4 copy.26
  66.6 0.4 copy.27
  67.0 0.0 slice-done
  67.1 0.0 slice-done.1
  67.1 1.3 slice-done.2
  68.4 7.6 %pad_maximum_fusion.wqkv_h = bf16[3,4096,768]{2,1,0:T(8,128)(2,1)} fusion(bf16[3,4096,128]{2,1,0:T(8,128)(2,1)S(1)} %bitcast.21, bf16[3,4096,128]{2,1,0:T(8,128)(2,1)S(1)} %bitcast.22, bf16[3,4096,512]{2,1,0:T(8,128)(2,1)S(1)} %bitcast.19), kind=kLoop, calls=%fused_computation | loop fusion | flops 56623104 | bytes 37748736 | tf_op jit(solution)/shard_map/concatenate | solution.py:452
  76.0 0.0 copy-done.1
  76.0 0.5 multiply_cosine_fusion
  76.5 0.1 maximum_bitcast_fusion
  76.7 0.7 pad_maximum_fusion.1.cs_h
  77.4 0.0 copy-done
  77.4 0.7 reshape.37.gain_v
  78.0 295.1 %decoder.1 = (bf16[256,4096]{1,0:T(8,128)(2,1)}, bf16[3,2,2,256,128]{4,3,2,1,0:T(8,128)(2,1)}) custom-call(bf16[256,4096]{1,0:T(8,128)(2,1)} %x_h.1, f32[2,256,128]{2,1,0:T(8,128)} %pad_maximum_fusion.1.cs_h, bf16[3,4096,768]{2,1,0:T(8,128)(2,1)} %pad_maximum_fusion.wqkv_h, bf16[3,1024,4096]{2,1,0:T(8,128)(2,1)} %bitcast.20, bf16[3,4096,3584]{2,1,0:T(8,128)(2,1)} %wg_h.1, ...), custom_call_target="tpu_custom_call" | custom-call | tf_op jit(solution)/shard_map/decoder/pallas_call | solution.py:472
  373.2 1.2 slice_bitcast_fusion
  374.3 1.2 copy.19
  375.5 1.1 copy.20
  376.6 3.1 copy.29
  (5 shorter events, 0.0 us)
Async XLA Ops:
  51.6 15.5 %slice-start = ((s8[12582912]{0:T(1024)(128)(4,1)}), s8[4194304]{0:T(1024)(128)(4,1)S(1)}, s32[]{:S(2)}) async-start(s8[12582912]{0:T(1024)(128)(4,1)} %bitcast.18), calls=%async_computation | async-start | bytes 8388608
  51.6 15.5 %slice-start.1 = ((s8[12582912]{0:T(1024)(128)(4,1)}), s8[4194304]{0:T(1024)(128)(4,1)S(1)}, s32[]{:S(2)}) async-start(s8[12582912]{0:T(1024)(128)(4,1)} %bitcast.18), calls=%async_computation.1 | async-start | bytes 8388608
  66.2 2.2 slice-start.2
  68.4 7.6 %copy-start.1 = (s32[256]{0:T(256)S(1)}, s32[256]{0:T(256)}, u32[]{:S(2)}) copy-start(s32[256]{0:T(256)} %param.11) | copy-start | bytes 3076
  68.4 9.0 %copy-start = (bf16[3,4096]{1,0:T(4,128)(2,1)S(1)}, bf16[3,4096]{1,0:T(4,128)(2,1)}, u32[]{:S(2)}) copy-start(bf16[3,4096]{1,0:T(4,128)(2,1)} %param.19) | copy-start | bytes 73732

commit v2 on v1

v2 whole, which is shorter than its diff:
```python
import functools
import math
import jax
import jax.numpy as jnp
from jax import lax
from jax.experimental import pallas as pl
from jax.experimental.pallas import tpu as pltpu
from jax.sharding import PartitionSpec as P

ROPE_BASE = 500000.0
EPS = 1e-5
F32 = jnp.float32
BF16 = jnp.bfloat16
MESH = pl.DeviceIdType.MESH

NSTREAM = 4
NGUBUF = 3
NWDBUF = 4
RATE = ((1, 1), (4, 3))
NAHEAD = 2
NRAW = 4


def rope_tables(positions, head_dim):
    half_dim = head_dim // 2
    inv_freq = ROPE_BASE ** (-(jnp.arange(half_dim, dtype=F32) * 2.0 / head_dim))
    angles = positions.astype(F32)[..., None] * inv_freq
    cos_t, sin_t = jnp.cos(angles), jnp.sin(angles)
    return jnp.stack([jnp.concatenate([cos_t, cos_t], -1), jnp.concatenate([-sin_t, sin_t], -1)])


def decoder_kernel(dims, x_h, cs_h, wq_h, wk_h, wv_h, wo_h, wg_h, wu_h, wd_h, gain_v, xout_h, kvout_h,
                   X, H, QKVS, Q, ATT, HID, G, PS, PAIR, RS, TAB, KV, GU, WD, WO, WQKV, MX, LS, ACC, RAW, WIDE,
                   s_xin, s_xs, s_xr, s_tab, s_gu, s_wd, s_wo, s_raw, s_ps, s_pr, s_rss, s_rsr, s_ags, s_agr,
                   s_fws, s_fwr, s_kvs, s_kvr, s_cl, s_cs, s_cr, s_out):
    L, T, D, NY, NX, GH, HD, FF, FT, BW = (dims[k] for k in ('L', 'T', 'D', 'NY', 'NX', 'GH', 'HD', 'FF', 'FT', 'BW'))
    NB = 2 * NY
    NGU = FF // FT
    QW = GH * HD
    NQ = (QW + 2 * HD) // (2 * HD)
    NS = NSTREAM
    R = T // NS
    NE = 5 * NS
    scale = 1.0 / math.sqrt(HD)

    y = lax.axis_index('head')
    s = lax.axis_index('seq')
    c = lax.rem(s, 2)
    xx = lax.div(s, 2)
    partner = {'seq': s + 1 - 2 * c}
    own0 = c * NY
    oth0 = (1 - c) * NY

    def rcopy(src, dst, ss, rs, dev):
        return pltpu.make_async_remote_copy(src_ref=src, dst_ref=dst, send_sem=ss, recv_sem=rs, device_id=dev, device_id_type=MESH)

    def lcopy(src, dst, sem):
        return pltpu.make_async_copy(src, dst, sem)

    def gu_copies(i):
        slot = lax.rem(i, NGUBUF)
        hs = lax.div(i, NGU)
        n = lax.rem(i, NGU)
        l = lax.div(hs, 2)
        cols = pl.ds(pl.multiple_of(c * FF + n * FT, FT), FT)
        return (lcopy(wg_h.at[l, :, cols], GU.at[slot, 0], s_gu.at[slot, 0]),
                lcopy(wu_h.at[l, :, cols], GU.at[slot, 1], s_gu.at[slot, 1]))

    assert NY == 4
    ya = y + 1 - 2 * lax.rem(y, 2)
    yb = NY - 1 - y
    y2 = lax.rem(y + 2, NY)

    def ring_block(n):
        return jnp.where(n == 0, y2, jnp.where(n == 1, ya, jnp.where(n == 2, yb, y)))

    def block_of(n):
        return jnp.where(n < NY, oth0, own0) + ring_block(lax.rem(n, NY))

    def wd_copy(i):
        slot = lax.rem(i, NWDBUF)
        hs = lax.div(i, NB)
        n = lax.rem(i, NB)
        l = lax.div(hs, 2)
        rows = pl.ds(pl.multiple_of(c * FF, FT), FF)
        cols = pl.ds(pl.multiple_of(block_of(n) * BW, BW), BW)
        return lcopy(wd_h.at[l, rows, cols], WD.at[slot], s_wd.at[slot])

    def wo_copy(l):
        return lcopy(wo_h.at[l, pl.ds(pl.multiple_of(c * QW, QW), QW), :], WO, s_wo.at[0])

    RP = RAW.shape[1]
    QROWS, KROWS = 2 * GH, 2
    NPQ, NPK = D * QROWS // RP, D * KROWS // RP

    def raw_copy(l, kind, n):
        ref, base = ((wq_h, 0), (wk_h, NPQ), (wv_h, NPQ + NPK))[kind]
        slot = lax.rem(base + n, NRAW)
        return lcopy(ref.at[l, pl.ds(pl.multiple_of(n * RP, RP), RP), :], RAW.at[slot], s_raw.at[slot])

    def raw_start(l, p):
        for kind, lo, hi in ((0, 0, NPQ), (1, NPQ, NPQ + NPK), (2, NPQ + NPK, NPQ + 2 * NPK)):
            @pl.when((p >= lo) & (p < hi))
            def _():
                raw_copy(l, kind, p - lo).start()

    def build_qkv(l, slot):
        for kind, lo, count in ((0, 0, NPQ), (1, NPQ, NPK), (2, NPQ + NPK, NPK)):
            heads, step = (GH, QROWS) if kind == 0 else (1, KROWS)
            kk = RP // step

            def body(n, carry):
                p = lo + n
                raw_copy(l, kind, n).wait()
                WIDE[...] = RAW[lax.rem(p, NRAW)].astype(F32)
                raw_start(l, p + NRAW)
                for h in range(heads):
                    col = h * HD if kind == 0 else QW + (kind - 1) * HD
                    WQKV[pl.ds(pl.multiple_of(n * kk, kk), kk), col:col + HD] = WIDE[pl.ds(c * heads + h, kk, stride=step), :].astype(BF16)
                slot(p)
                return carry
            lax.fori_loop(0, count, body, 0)

    for p in range(NRAW):
        raw_start(0, jnp.int32(p))

    barrier = pltpu.get_barrier_semaphore()
    peers = [partner, {'head': ya}, {'head': yb}]
    peers += [{'seq': lax.rem(s + 2 * d, 2 * NX)} for d in range(1, NX)]
    for peer in peers:
        pl.semaphore_signal(barrier, inc=1, device_id=peer, device_id_type=MESH)
    pl.semaphore_wait(barrier, len(peers))

    def xin_local(b):
        return lcopy(x_h.at[:, pl.ds(b * BW, BW)], X.at[c, b], s_xin.at[b])

    def xin_remote(b):
        return rcopy(x_h.at[:, pl.ds(b * BW, BW)], X.at[c, b], s_xs.at[b], s_xr.at[b], partner)

    def tab_local():
        return lcopy(cs_h, TAB.at[c], s_tab.at[0])

    def tab_remote():
        return rcopy(cs_h, TAB.at[c], s_tab.at[1], s_tab.at[2], partner)

    for b in range(NB):
        xin_remote(b).start()
        xin_local(b).start()
    tab_remote().start()
    tab_local().start()
    build_qkv(0, lambda k: None)
    for i in range(NGUBUF):
        for cp in gu_copies(jnp.int32(i)):
            cp.start()
    for i in range(NWDBUF):
        wd_copy(jnp.int32(i)).start()
    wo_copy(0).start()
    for b in range(NB):
        xin_local(b).wait()
        xin_remote(b).wait()
    tab_local().wait()
    tab_remote().wait()

    def rows_of(st):
        return pl.ds(pl.multiple_of(st * R, R), R)

    def side(st, first):
        return jnp.where(lax.rem(st, 2) == (0 if first else 1), ya, yb)

    def pair_copy(j, bb):
        return rcopy(PS.at[j, oth0 + bb], PAIR.at[j, bb], s_ps.at[j, bb], s_pr.at[j, bb], partner)

    def rs_copy(j, t, st):
        dev = side(st, t < 2)
        src = y2 if t == 1 else dev
        return rcopy(PS.at[j, own0 + src, rows_of(st)], RS.at[j, t, rows_of(st)],
                     s_rss.at[j, t, st], s_rsr.at[j, t, st], {'head': dev})

    def ag_copy(j, t, st):
        src = side(st, False) if t == 2 else y
        ref = X.at[j, own0 + src, rows_of(st)]
        return rcopy(ref, ref, s_ags.at[j, t, st], s_agr.at[j, t, st], {'head': side(st, t > 0)})

    def fw_copy(j, t, st):
        src = (y, side(st, False), side(st, True), y2)[t]
        ref = X.at[j, own0 + src, rows_of(st)]
        return rcopy(ref, ref, s_fws.at[j, t, st], s_fwr.at[j, t, st], partner)

    def service(j, e):
        kind = lax.div(e, NS)
        st = lax.rem(e, NS)
        rows = rows_of(st)

        @pl.when(kind < 3)
        def _():
            @pl.when(kind == 0)
            def _():
                @pl.when(st == 0)
                def _():
                    pair_copy(j, y2).wait_recv()
                    pair_copy(j, ya).wait_recv()

                @pl.when(st == 1)
                def _():
                    pair_copy(j, yb).wait_recv()
                PS[j, own0 + y2, rows] += PAIR[j, y2, rows]
                rs_copy(j, 1, st).start()
                blk = side(st, True)
                PS[j, own0 + blk, rows] += PAIR[j, blk, rows]
                rs_copy(j, 0, st).start()

            @pl.when(kind == 1)
            def _():
                rs_copy(j, 1, st).wait_recv()
                blk = side(st, False)
                PS[j, own0 + blk, rows] = PS[j, own0 + blk, rows] + PAIR[j, blk, rows] + RS[j, 1, rows]
                rs_copy(j, 2, st).start()

            @pl.when(kind == 2)
            def _():
                @pl.when(st == 0)
                def _():
                    pair_copy(j, y).wait_recv()
                rs_copy(j, 0, st).wait_recv()
                rs_copy(j, 2, st).wait_recv()
                total = (PS[j, own0 + y, rows] + PAIR[j, y, rows]) + (RS[j, 0, rows] + RS[j, 2, rows])
                upd = total.astype(BF16).astype(F32)
                X[j, own0 + y, rows] = (X[j, own0 + y, rows].astype(F32) + upd).astype(BF16)
                ag_copy(j, 0, st).start()
                ag_copy(j, 1, st).start()
                fw_copy(j, 0, st).start()

        @pl.when(kind >= 3)
        def _():
            @pl.when(kind == 3)
            def _():
                ag_copy(j, 0, st).wait_recv()
                ag_copy(j, 2, st).start()
                fw_copy(j, 1, st).start()

            @pl.when(kind == 4)
            def _():
                ag_copy(j, 1, st).wait_recv()
                fw_copy(j, 2, st).start()
                ag_copy(j, 2, st).wait_recv()
                fw_copy(j, 3, st).start()

    def run_events(j, lo, hi):
        def body(e, carry):
            service(j, e)
            return carry
        lax.fori_loop(lo, hi, body, 0)

    def norm_rows(j, l, st):
        rows = rows_of(st)
        ssq = jnp.zeros((R, BW), F32)
        for b in range(NB):
            xb = X[j, b, rows, :].astype(F32)
            ssq = ssq + xb * xb
        inv = lax.rsqrt(jnp.sum(ssq, axis=-1, keepdims=True) * (1.0 / D) + EPS)
        for b in range(NB):
            xb = X[j, b, rows, :].astype(F32)
            H[rows, b * BW:(b + 1) * BW] = (xb * inv * gain_v[l, :, b * BW:(b + 1) * BW]).astype(BF16)

    def norm(j, l):
        def body(st, carry):
            norm_rows(j, l, st)
            return carry
        lax.fori_loop(0, NS, body, 0)

    def drain(j, e0, l_next):
        run_events(j, e0, NE)

        def arrive(st, carry):
            for t in range(NY):
                fw_copy(j, t, st).wait_recv()

            @pl.when(l_next < L)
            def _():
                norm_rows(j, l_next, st)
            return carry
        lax.fori_loop(0, NS, arrive, 0)
        for bb in range(NY):
            pair_copy(j, bb).wait_send()

        def ends(st, carry):
            for t in range(NY - 1):
                rs_copy(j, t, st).wait_send()
                ag_copy(j, t, st).wait_send()
            for t in range(NY):
                fw_copy(j, t, st).wait_send()
            return carry
        lax.fori_loop(0, NS, ends, 0)

    def push_copy(j, l, d):
        g = 2 * xx + j
        return rcopy(KV.at[l, g], KV.at[l, g], s_kvs.at[j, d - 1], s_kvr.at[l * (2 * NX) + g], {'seq': lax.rem(s + 2 * d, 2 * NX)})

    def recv_wait(l, g):
        rcopy(KV.at[l, g], KV.at[l, g], s_kvs.at[0, 0], s_kvr.at[l * (2 * NX) + g], partner).wait_recv()

    def cache_local(l, j):
        return lcopy(KV.at[l, 2 * xx + j], kvout_h.at[l, c], s_cl.at[l])

    def cache_remote(l, j):
        return rcopy(KV.at[l, 2 * xx + j], kvout_h.at[l, c], s_cs.at[l], s_cr.at[l], partner)

    def qkv(j, l, slot):
        for n in range(NQ):
            QKVS[n] = jnp.dot(H[...], WQKV[:, n * 2 * HD:(n + 1) * 2 * HD], preferred_element_type=F32).astype(BF16)
        slot(0)
        g = 2 * xx + j

        def rot(val):
            vf = val.astype(F32)
            return (vf * TAB[j, 0] + pltpu.roll(vf, HD // 2, 1) * TAB[j, 1]).astype(BF16)
        KV[l, g, 0] = rot(QKVS[NQ - 1, :, 0:HD])
        KV[l, g, 1] = QKVS[NQ - 1, :, HD:2 * HD]
        for d in range(1, NX):
            @pl.when(xx + d < NX)
            def _():
                push_copy(j, l, d).start()

        @pl.when(c == j)
        def _():
            cache_local(l, j).start()

        @pl.when(c != j)
        def _():
            cache_remote(l, j).start()
        for h in range(GH):
            Q[j, h] = rot(QKVS[h // 2, :, (h % 2) * HD:(h % 2 + 1) * HD])

    def push_done(j, l):
        for d in range(1, NX):
            @pl.when(xx + d < NX)
            def _():
                push_copy(j, l, d).wait_send()

    def attention(j, l, slot):
        g = 2 * xx + j
        nt = (((1,), (1,)), ((), ()))
        QB = T // 2
        ex = scale * math.log2(math.e)

        row_i = lax.broadcasted_iota(jnp.int32, (QB, T), 0)
        col_i = lax.broadcasted_iota(jnp.int32, (QB, T), 1)

        def logits(h, qs, gi):
            return lax.dot_general(Q[j, h, qs], KV[l, gi, 0], nt, preferred_element_type=F32) * ex

        def rowmax(parts):
            top = parts[0]
            for part in parts[1:]:
                top = jnp.maximum(top, part)
            return jnp.max(top, axis=1, keepdims=True)

        def weigh(parts, m, gs):
            probs = [jnp.exp2(part - m) for part in parts]
            tot = probs[0]
            for part in probs[1:]:
                tot = tot + part
            out = jnp.dot(probs[0].astype(BF16), KV[l, gs[0], 1], preferred_element_type=F32)
            for part, gi in zip(probs[1:], gs[1:]):
                out = out + jnp.dot(part.astype(BF16), KV[l, gi, 1], preferred_element_type=F32)
            return jnp.sum(tot, axis=1, keepdims=True), out

        for h in range(GH):
            for q0 in range(0, T, QB):
                qs = slice(q0, q0 + QB)
                gs = [g - 1, g] if j == 1 else [g]
                parts = [logits(h, qs, gi) for gi in gs]
                parts[-1] = jnp.where(row_i + q0 >= col_i, parts[-1], -jnp.inf)
                m = rowmax(parts)
                tot, out = weigh(parts, m, gs)
                MX[h, qs] = jnp.broadcast_to(m, (QB, HD))
                LS[h, qs] = jnp.broadcast_to(tot, (QB, HD))
                ACC[h, qs] = out
        slot(0)

        def body(i, carry):
            gs = [2 * i, 2 * i + 1]
            if j == 0:
                for gi in gs:
                    recv_wait(l, gi)
            for h in range(GH):
                for q0 in range(0, T, QB):
                    qs = slice(q0, q0 + QB)
                    parts = [logits(h, qs, gi) for gi in gs]
                    m_old = MX[h, qs]
                    m_new = jnp.maximum(m_old, rowmax(parts))
                    tot, out = weigh(parts, jnp.concatenate([m_new] * (T // HD), axis=1), gs)
                    alpha = jnp.exp2(m_old - m_new)
                    MX[h, qs] = m_new
                    LS[h, qs] = LS[h, qs] * alpha + tot
                    ACC[h, qs] = ACC[h, qs] * alpha + out
            slot(i + 1)
            return carry
        lax.fori_loop(0, xx, body, 0)
        for h in range(GH):
            ATT[:, h * HD:(h + 1) * HD] = (ACC[h] / LS[h]).astype(BF16)

    def gate_up(j, l, n0, n1, slot):
        def act(n):
            gate = G[0]
            HID[:, pl.ds(pl.multiple_of(n * FT, FT), FT)] = (gate * jax.nn.sigmoid(gate) * G[1]).astype(BF16)

        def body(n, carry):
            i = (2 * l + j) * NGU + n
            sl = lax.rem(i, NGUBUF)
            for cp in gu_copies(i):
                cp.wait()
            act(jnp.maximum(n - 1, n0))
            for k in range(2):
                G[k] = jnp.dot(H[...], GU[sl, k], preferred_element_type=F32)

            @pl.when(n + NGUBUF < NGU)
            def _():
                for cp in gu_copies(i + NGUBUF):
                    cp.start()
            slot(n - n0)
            return carry
        lax.fori_loop(n0, n1, body, 0)
        act(n1 - 1)

    def o_tile(blk):
        cols = pl.ds(pl.multiple_of(blk * BW, BW), BW)
        return jnp.dot(ATT[...], WO[:, cols], preferred_element_type=F32)

    def send_pair(j, n):
        @pl.when(n < NY)
        def _():
            pair_copy(j, ring_block(n)).start()

    def down(j, l, with_o, slot):
        def body(m, carry):
            i = (2 * l + j) * NB + 2 * m
            for k in range(2):
                wd_copy(i + k).wait()
            for k in range(2):
                blk = block_of(2 * m + k)
                val = jnp.dot(HID[...], WD[lax.rem(i + k, NWDBUF)], preferred_element_type=F32)
                if with_o:
                    val = val + o_tile(blk)
                PS[j, blk] = val

            @pl.when(i + NWDBUF < 2 * L * NB)
            def _():
                for k in range(2):
                    wd_copy(i + NWDBUF + k).start()
            k0 = m - (NB // 2 - NGUBUF)

            @pl.when((k0 >= 0) & (2 * l + j + 1 < 2 * L))
            def _():
                for cp in gu_copies((2 * l + j + 1) * NGU + k0):
                    cp.start()
            if with_o:
                for k in range(2):
                    send_pair(j, 2 * m + k)
            slot(m)
            return carry
        lax.fori_loop(0, NB // 2, body, 0)

    def o_proj(j, l):
        def body(m, carry):
            for k in range(2):
                blk = block_of(2 * m + k)
                PS[j, blk] += o_tile(blk)
            for k in range(2):
                send_pair(j, 2 * m + k)
            return carry
        lax.fori_loop(0, NB // 2, body, 0)

    def layer(l, carry):
        def events(j, first):
            num, den = RATE[j]
            e_first = NS if (j == 1) else 0

            def slot(k):
                kk = first + k
                lo = jnp.minimum(e_first + lax.div(kk * num, den), NE)
                hi = jnp.minimum(e_first + lax.div((kk + 1) * num, den), NE)
                if j == 1:
                    hi = jnp.where(l > 0, hi, lo)
                run_events(j, lo, hi)
            return slot

        def reached(j, k):
            return jnp.minimum((NS if j == 1 else 0) + lax.div(k * RATE[j][0], RATE[j][1]), NE)

        qkv(0, l, events(1, 0))
        gate_up(0, l, 0, NGU, events(1, 1))
        down(0, l, False, events(1, 1 + NGU))

        @pl.when(l > 0)
        def _():
            drain(1, reached(1, jnp.int32(1 + NGU + NB // 2)), l)

        @pl.when(l == 0)
        def _():
            norm(1, l)

        qkv(1, l, lambda k: None)

        @pl.when(l + 1 < L)
        def _():
            for p in range(NRAW):
                raw_start(l + 1, jnp.int32(p))
        if NAHEAD:
            gate_up(1, l, 0, NAHEAD, lambda k: None)
        attention(0, l, lambda k: None)
        wo_copy(l).wait()
        o_proj(0, l)

        gate_up(1, l, NAHEAD, NGU, events(0, 0))
        k0 = NGU - NAHEAD
        attention(1, l, events(0, k0))
        k0 = k0 + xx + 1
        down(1, l, True, events(0, k0))
        e0 = reached(0, k0 + NB // 2)

        @pl.when(l + 1 < L)
        def _():
            wo_copy(l + 1).start()

            def one(k):
                lo = jnp.minimum(e0 + k, NE)
                run_events(0, lo, jnp.minimum(lo + 1, NE))
            build_qkv(l + 1, one)
        run_events(1, 0, NS)
        drain(0, jnp.minimum(jnp.where(l + 1 < L, e0 + NPQ + 2 * NPK, e0), NE), l + 1)
        push_done(0, l)
        push_done(1, l)
        return carry

    norm(0, 0)
    lax.fori_loop(0, L, layer, 0)
    drain(1, NS, L)

    for b in range(NB):
        lcopy(X.at[c, b], xout_h.at[:, pl.ds(b * BW, BW)], s_out.at[b]).start()
    for b in range(NB):
        lcopy(X.at[c, b], xout_h.at[:, pl.ds(b * BW, BW)], s_out.at[b]).wait()
    for l in range(L):
        cache_local(l, 0).wait()
        cache_remote(l, 0).wait()


def solution(mesh):
    NY = mesh.shape['head']
    NX = mesh.shape['seq'] // 2
    row_spec = P(('batch', 'seq'), None)
    pos_spec = P(('batch', 'seq'))
    head_spec = P(None, None, 'head', None)
    out_proj_spec = P(None, 'head', None, None)
    col_spec = P(None, None, 'head')
    down_spec = P(None, 'head', None)
    cache_spec = P(None, ('batch', 'seq'), 'head', None)

    def local_forward(x_loc, pos_loc, w_q, w_k, w_v, w_o, w_gate, w_up, w_down, norm_gain):
        T, D = x_loc.shape
        L, _, q_local, HD = w_q.shape
        GH = q_local // 2
        FF = w_gate.shape[2] // 2
        BW = D // (2 * NY)
        FT = 256 if FF % 256 == 0 else 128
        dims = dict(L=L, T=T, D=D, NY=NY, NX=NX, GH=GH, HD=HD, FF=FF, FT=FT, BW=BW)
        wq = w_q.reshape(L, D * q_local, HD)
        wk = w_k.reshape(L, D * 2, HD)
        wv = w_v.reshape(L, D * 2, HD)
        wo = w_o.reshape(L, q_local * HD, D)
        gain = norm_gain.astype(F32).reshape(L, 1, D)
        tab = rope_tables(pos_loc, HD)
        QW = GH * HD
        NB = 2 * NY
        NQ = (QW + 2 * HD) // (2 * HD)
        RP = min(2048, D * 2)
        any_spec = pl.BlockSpec(memory_space=pl.ANY)
        dma = pltpu.SemaphoreType.DMA
        V = pltpu.VMEM
        scratch = [
            V((2, NB, T, BW), BF16), V((T, D), BF16), V((NQ, T, 2 * HD), BF16), V((2, GH, T, HD), BF16), V((T, QW), BF16),
            V((T, FF), BF16), V((2, T, FT), F32), V((2, NB, T, BW), F32), V((2, NY, T, BW), F32), V((2, NY - 1, T, BW), F32),
            V((2, 2, T, HD), F32), V((L, 2 * NX, 2, T, HD), BF16), V((NGUBUF, 2, D, FT), BF16), V((NWDBUF, FF, BW), BF16),
            V((QW, D), BF16), V((D, QW + 2 * HD), BF16), V((GH, T, HD), F32), V((GH, T, HD), F32), V((GH, T, HD), F32),
            V((NRAW, RP, HD), BF16), V((RP, HD), F32),
            dma((NB,)), dma((NB,)), dma((NB,)), dma((3,)), dma((NGUBUF, 2)), dma((NWDBUF,)), dma((1,)), dma((NRAW,)),
            dma((2, NY)), dma((2, NY)), dma((2, NY - 1, NSTREAM)), dma((2, NY - 1, NSTREAM)),
            dma((2, NY - 1, NSTREAM)), dma((2, NY - 1, NSTREAM)), dma((2, NY, NSTREAM)), dma((2, NY, NSTREAM)),
            dma((2, NX)), dma((L * 2 * NX,)), dma((L,)), dma((L,)), dma((L,)), dma((NB,)),
        ]
        x_out, kv = pl.pallas_call(
            functools.partial(decoder_kernel, dims),
            out_shape=(jax.ShapeDtypeStruct((T, D), BF16), jax.ShapeDtypeStruct((L, 2, 2, T, HD), BF16)),
            in_specs=[any_spec] * 9 + [pl.BlockSpec(memory_space=pltpu.VMEM)],
            out_specs=(any_spec, any_spec),
            scratch_shapes=scratch,
            compiler_params=pltpu.CompilerParams(collective_id=0, has_side_effects=True, vmem_limit_bytes=67043328),
            name='decoder',
        )(x_loc, tab, wq, wk, wv, wo, w_gate, w_up, w_down, gain)
        kv = jnp.transpose(kv, (2, 0, 3, 1, 4))
        return x_out, kv[0], kv[1]

    return jax.shard_map(local_forward, mesh=mesh, in_specs=(row_spec, pos_spec, head_spec, head_spec, head_spec, out_proj_spec, col_spec, col_spec, down_spec, P(None, None)), out_specs=(row_spec, cache_spec, cache_spec), check_vma=False)
```

time: 381 us -> 299 us (0.78)
  local copies, waits for them, and re-layouts: 75 us -> 8.01 us
  Pallas kernels: 295 us -> 287 us
  other arithmetic: 8.97 us -> 2.08 us
    dynamic_slice x2 -> x0, local copies, waits for them, and re-layouts: 29 us -> none  [the longest x1 14.6 us: local_forward(): wv_c = lax.dynamic_slice_in_dim(w_v, core, 1, 2).reshape(L, D, HD)]
    unnamed x16 -> x3, local copies, waits for them, and re-layouts: 27.6 us -> 5.43 us
    reshape x1 -> x0, local copies, waits for them, and re-layouts: 16.6 us -> none  [local_forward(): lax.dynamic_slice_in_dim(w_q, core * GH, GH, 2).reshape(L, D, GH * HD)]
    pallas_call x1, Pallas kernels: 295 us -> 287 us  [local_forward(): pl.pallas_call(functools.partial(decoder_kernel, dims), out_shape=(jax.Sh...]
    concatenate x1 -> x0, other arithmetic: 7.56 us -> none  [local_forward(): wqkv = jnp.concatenate([wq_c, wk_c, wv_c], axis=2)]
where the time goes in v2:
time: 299 us; the launch traced here: 298 us
  Pallas kernels  287 us (96%)
  local copies, waits for them, and re-layouts  8.01 us (3%)
    pallas_call x1, Pallas kernels, local_forward(): pl.pallas_call(functools.partial(decoder_kernel, dims), out_shape=(jax.Sh...  287 us

profile of v2, /device:TPU:103, one launch (start us, length us, event | category | flops | bytes accessed | tf_op | source)
XLA Modules:
  0.0 298.0 jit_solution(7422321044454548469)
XLA Ops:
  0.6 0.7 convert_element_type.4
  1.3 1.4 reshape.37.gain_v
  2.7 0.5 multiply_cosine_fusion
  3.3 0.1 maximum_bitcast_fusion
  3.4 0.7 pad_maximum_fusion.cs_h
  4.1 287.3 %decoder.1 = (bf16[256,4096]{1,0:T(8,128)(2,1)}, bf16[3,2,2,256,128]{4,3,2,1,0:T(8,128)(2,1)}) custom-call(bf16[256,4096]{1,0:T(8,128)(2,1)} %x_h.1, f32[2,256,128]{2,1,0:T(8,128)} %pad_maximum_fusion.cs_h, bf16[3,32768,128]{2,1,0:T(8,128)(2,1)} %bitcast.13, bf16[3,8192,128]{2,1,0:T(8,128)(2,1)} %bitcast.15, bf16[3,8192,128]{2,1,0:T(8,128)(2,1)} %bitcast.16, ...), custom_call_target="tpu_custom_call" | custom-call | tf_op jit(solution)/shard_map/decoder/pallas_call | solution.py:592
  291.4 1.2 slice_bitcast_fusion
  292.6 1.2 copy.14
  293.8 1.1 copy.13
  294.9 3.1 %copy.16 = bf16[256,4096]{1,0:T(8,128)(2,1)} copy(bf16[256,4096]{1,0:T(8,128)(2,1)} %get-tuple-element.20) | data formatting | bytes 4194304
  (1 shorter events, 0.0 us)
